TPU v7x, 32 devices: a whole 2x2x4 slice. The times are simulated.
32 devices in a mesh: dp: 16 (over z, y, core), tensor: 2 (over x).
Axes of the slice: x: 2, y: 2, z: 4, core: 2. Of those that a mesh axis runs over, the one named last changes fastest.
Arguments:
- token_ids: int32 [8192], P('dp'), may hold values from 0 to 30719
- lengths: int32 [16], P('dp'), may hold values from 128 to 512
- word_table: bfloat16 [30720, 1024], P('tensor'), may hold values from -6 to 6
- pos_table: bfloat16 [512, 1024], replicated, may hold values from -4 to 4
- w_qkv: bfloat16 [2, 3, 1024, 1024], P(None, None, 'dp', 'tensor'), may hold values from -0.1875 to 0.1875
- w_out: bfloat16 [2, 1024, 1024], P(None, 'dp', 'tensor'), may hold values from -0.1875 to 0.1875
- w_up: bfloat16 [2, 1024, 4096], P(None, 'dp', 'tensor'), may hold values from -0.1875 to 0.1875
- w_down: bfloat16 [2, 1024, 4096], P(None, 'dp', 'tensor'), may hold values from -0.09375 to 0.09375
- up_bias: float32 [2, 4096], P(None, 'tensor'), may hold values from -3 to 3
- dense_bias: float32 [2, 2, 1024], replicated, may hold values from -3 to 3
- norm_gain: float32 [5, 1024], replicated, may hold values from 0.1 to 1.9
- norm_bias: float32 [5, 1024], replicated, may hold values from -3 to 3
Outputs:
- encoded: bfloat16 [8192, 1024], P('dp', 'tensor')
- similarity: float32 [16, 16], P('dp')
All inputs are finite; a program needn't handle non-finite values.
Results may differ from a plain program's by a relative error of at most 0.015.
Values may be sent and summed in bfloat16 or wider, within the bound.
A program may use at most 128 MiB of HBM per device.

v0:
```python
import jax
import jax.numpy as jnp
from jax import lax
from jax.sharding import PartitionSpec as P

D = 1024
BLOCK = 512
LAYERS = 2
HEAD = 64
EPS = 1e-05


def layer_norm(values, gain, shift):
    average = jnp.mean(values, axis=-1, keepdims=True)
    centered = values - average
    spread = jnp.mean(centered * centered, axis=-1, keepdims=True)
    return centered * lax.rsqrt(spread + EPS) * gain + shift


def settle(partial_value, residual, bias_row, gain, shift, which):
    if which == 0:
        summed = lax.psum(partial_value, "tensor").astype(jnp.float32)
    else:
        summed = lax.psum(partial_value, "tensor").astype(jnp.float32)
    return layer_norm(residual.astype(jnp.float32) + summed + bias_row, gain, shift).astype(
        jnp.bfloat16
    )


def project_back(left, weight):
    product = lax.dot_general(
        left, weight, (((1,), (1,)), ((), ())), preferred_element_type=jnp.float32
    )
    return product.astype(jnp.bfloat16)


def per_device(
    token_ids,
    lengths,
    word_table,
    pos_table,
    w_qkv,
    w_out,
    w_up,
    w_down,
    up_bias,
    dense_bias,
    norm_gain,
    norm_bias,
):
    passage_count = lengths.shape[0]
    vocab_rows = word_table.shape[0]
    local_ids = token_ids - lax.axis_index("tensor") * vocab_rows
    inside = (local_ids >= 0) & (local_ids < vocab_rows)
    picked = jnp.take(word_table, jnp.clip(local_ids, 0, vocab_rows - 1), axis=0)
    picked = jnp.where(inside[:, None], picked, jnp.zeros_like(picked))
    embedded = lax.psum(picked, "tensor").astype(jnp.float32)
    embedded = embedded.reshape(passage_count, BLOCK, D) + pos_table.astype(jnp.float32)[None]
    hidden = layer_norm(
        embedded.reshape(passage_count * BLOCK, D), norm_gain[0], norm_bias[0]
    ).astype(jnp.bfloat16)
    visible = jnp.arange(BLOCK, dtype=jnp.int32)[None, :] < lengths[:, None]
    local_heads = w_qkv.shape[3] // HEAD
    scale_dot = 1.0 / jnp.sqrt(jnp.float32(HEAD))
    for layer in range(LAYERS):
        columns = hidden
        projected = jnp.einsum(
            "td,idc->itc",
            columns,
            lax.all_gather(w_qkv[layer], "dp", axis=1, tiled=True),
            preferred_element_type=jnp.float32,
        )
        projected = projected.astype(jnp.bfloat16).reshape(
            3, passage_count, BLOCK, local_heads, HEAD
        )
        scores = (
            jnp.einsum(
                "cqhe,ckhe->chqk", projected[0], projected[1], preferred_element_type=jnp.float32
            )
            * scale_dot
        )
        scores = jnp.where(visible[:, None, None, :], scores, jnp.float32(-1e30))
        top = jnp.max(scores, axis=-1, keepdims=True)
        expo = jnp.exp(scores - top)
        weights_soft = (expo / jnp.sum(expo, axis=-1, keepdims=True)).astype(jnp.bfloat16)
        context = jnp.einsum(
            "chqk,ckhe->cqhe", weights_soft, projected[2], preferred_element_type=jnp.float32
        )
        context = context.astype(jnp.bfloat16).reshape(passage_count * BLOCK, local_heads * HEAD)
        attended = project_back(context, lax.all_gather(w_out[layer], "dp", axis=0, tiled=True))
        middle = settle(
            attended,
            hidden,
            dense_bias[layer, 0],
            norm_gain[2 * layer + 1],
            norm_bias[2 * layer + 1],
            0,
        )
        raised = jnp.dot(
            middle,
            lax.all_gather(w_up[layer], "dp", axis=0, tiled=True),
            preferred_element_type=jnp.float32,
        )
        inner = jax.nn.gelu(raised + up_bias[layer], approximate=False).astype(jnp.bfloat16)
        mlp_out = project_back(inner, lax.all_gather(w_down[layer], "dp", axis=0, tiled=True))
        hidden = settle(
            mlp_out,
            middle,
            dense_bias[layer, 1],
            norm_gain[2 * layer + 2],
            norm_bias[2 * layer + 2],
            1,
        )
    width_share = hidden.shape[1] // lax.axis_size("tensor")
    encoded = lax.dynamic_slice_in_dim(
        hidden, lax.axis_index("tensor") * width_share, width_share, 1
    )
    weights_pool = visible.astype(jnp.float32)
    states = hidden.reshape(passage_count, BLOCK, D).astype(jnp.float32)
    pooled = (
        jnp.sum(weights_pool[:, :, None] * states, axis=1) / lengths.astype(jnp.float32)[:, None]
    )
    unit = pooled * lax.rsqrt(jnp.sum(pooled * pooled, axis=1, keepdims=True) + 1e-06)
    every_unit = lax.all_gather(unit, "dp", axis=0, tiled=True)
    similarity = jnp.dot(
        unit, every_unit.T, precision=lax.Precision.HIGHEST, preferred_element_type=jnp.float32
    )
    return (encoded, similarity)


def solution(mesh):
    in_specs = (
        P("dp"),
        P("dp"),
        P("tensor", None),
        P(),
        P(None, None, "dp", "tensor"),
        P(None, "dp", "tensor"),
        P(None, "dp", "tensor"),
        P(None, "dp", "tensor"),
        P(None, "tensor"),
        P(),
        P(),
        P(),
    )
    out_specs = (P("dp", "tensor"), P("dp", None))
    return jax.shard_map(
        per_device, mesh=mesh, in_specs=in_specs, out_specs=out_specs, check_vma=False
    )
```

profile of v0, /device:TPU:0, one launch (start us, length us, event | category | flops | bytes accessed | tf_op | source)
XLA Modules:
  0.0 518.2 jit_solution(6977902281912645279)
XLA Ops:
  8.0 0.7 compare_and_fusion
  8.8 12.5 %gather_fusion = bf16[512,1024]{1,0:T(8,128)(2,1)S(1)} fusion(bf16[15360,1024]{1,0:T(8,128)(2,1)} %param.14, s32[1024]{0:T(1024)S(1)} %pad_clamp_fusion), kind=kCustom, calls=%fused_computation | custom fusion | bytes 2099200 | tf_op jit(solution)/shard_map/jit(_take)/gather | solution.py:55
  21.3 1.2 select_select_fusion
  22.6 0.8 fusion.159
  23.5 0.7 fusion.160
  24.9 40.1 %all-reduce.6.cloned.1.call-done = bf16[512,1024]{1,0:T(8,128)(2,1)} async-done(((bf16[512,1024]{1,0:T(8,128)(2,1)}), bf16[512,1024]{1,0:T(8,128)(2,1)}) %all-reduce.6.cloned.1.call-update) | async-done | bytes 1048592 | tf_op jit(solution)/shard_map/psum | solution.py:57
  65.1 1.7 fusion.49
  66.7 1.7 multiply_reduce_fusion.5
  69.0 4.2 all-gather.18.cloned.1.call-done
  73.2 3.7 fusion.67
  77.1 5.3 %fusion.165 = (f32[8,512]{1,0:T(8,128)S(1)}, f32[8,512,512]{1,2,0:T(8,128)}) fusion(pred[512]{0:T(512)(128)(4,1)S(1)} %iota_compare_fusion, bf16[512,8,64]{0,2,1:T(8,128)(2,1)S(1)} %bitcast.119, bf16[512,8,64]{0,2,1:T(8,128)(2,1)S(1)} %bitcast.118), kind=kOutput, calls=%fused_computation.202 | convolution fusion | flops 276824576 | bytes 9454080 | tf_op jit(solution)/shard_map/sub | solution.py:84
  82.4 4.2 fusion.81
  86.7 24.9 %all-gather.20.cloned.1.call-done = bf16[1,1024,512]{2,1,0:T(8,128)(2,1)} async-done(((bf16[1,64,512]{2,1,0:T(8,128)(2,1)}), bf16[1,1024,512]{2,1,0:T(8,128)(2,1)}) %all-gather.20.cloned.1.call-update) | async-done | bytes 1048592 | tf_op jit(solution)/shard_map/all_gather | solution.py:90
  111.6 3.0 convolution_convert_fusion.1
  114.6 0.8 fusion.157
  115.6 0.8 fusion.158
  116.7 37.1 %all-reduce.8.cloned.1.call-done = bf16[512,1024]{1,0:T(8,128)(2,1)} async-done(((bf16[512,1024]{1,0:T(8,128)(2,1)}), bf16[512,1024]{1,0:T(8,128)(2,1)}) %all-reduce.8.cloned.1.call-update) | async-done | bytes 1048592 | tf_op jit(solution)/shard_map/psum | solution.py:22
  153.8 1.7 fusion.56
  155.6 1.8 multiply_reduce_fusion.4
  158.0 8.5 %all-gather.22.cloned.1.call-done = bf16[1,1024,2048]{2,1,0:T(8,128)(2,1)} async-done(((bf16[1,64,2048]{2,1,0:T(8,128)(2,1)}), bf16[1,1024,2048]{2,1,0:T(8,128)(2,1)}) %all-gather.22.cloned.1.call-update) | async-done | bytes 4194320 | tf_op jit(solution)/shard_map/all_gather | solution.py:101
  166.5 51.6 %all-gather.24.cloned.1.call-done = bf16[1,1024,2048]{2,1,0:T(8,128)(2,1)} async-done(((bf16[1,64,2048]{2,1,0:T(8,128)(2,1)}), bf16[1,1024,2048]{2,1,0:T(8,128)(2,1)}) %all-gather.24.cloned.1.call-update) | async-done | bytes 4194320 | tf_op jit(solution)/shard_map/all_gather | solution.py:105
  218.2 16.7 %fusion.70 = bf16[512,1024]{1,0:T(8,128)(2,1)} fusion(bf16[1,1024,2048]{2,1,0:T(8,128)(2,1)} %all-gather.24.cloned.1.call-done, bf16[512,1024]{1,0:T(8,128)(2,1)S(1)} %add_convert_fusion.3, bf16[1,1024,2048]{2,1,0:T(8,128)(2,1)} %all-gather.22.cloned.1.call-done, f32[2048]{0:T(1024)S(1)} %bitcast.144), kind=kOutput, calls=%fused_computation.97 | convolution fusion | flops 4364697600 | bytes 10493952 | tf_op jit(solution)/shard_map/dot_general | solution.py:31
  235.0 0.7 all-gather.26.cloned.1.call-update
  235.7 0.7 all-gather.28.cloned.1.call-update
  236.5 37.3 %all-reduce.10.cloned.1.call-done = bf16[512,1024]{1,0:T(8,128)(2,1)} async-done(((bf16[512,1024]{1,0:T(8,128)(2,1)}), bf16[512,1024]{1,0:T(8,128)(2,1)}) %all-reduce.10.cloned.1.call-update) | async-done | bytes 1048592 | tf_op jit(solution)/shard_map/psum | solution.py:24
  273.7 1.8 fusion.57
  275.5 1.8 multiply_reduce_fusion.3
  277.9 3.7 all-gather.26.cloned.1.call-done
  281.6 3.7 fusion.64
  285.5 5.3 %fusion.166 = (f32[8,512]{1,0:T(8,128)S(1)}, f32[8,512,512]{1,2,0:T(8,128)}) fusion(pred[512]{0:T(512)(128)(4,1)S(1)} %iota_compare_fusion, bf16[512,8,64]{0,2,1:T(8,128)(2,1)S(1)} %bitcast.117, bf16[512,8,64]{0,2,1:T(8,128)(2,1)S(1)} %bitcast.116), kind=kOutput, calls=%fused_computation.203 | convolution fusion | flops 276824576 | bytes 9454080 | tf_op jit(solution)/shard_map/sub | solution.py:84
  290.8 4.2 fusion.80
  295.0 25.1 %all-gather.28.cloned.1.call-done = bf16[1,1024,512]{2,1,0:T(8,128)(2,1)} async-done(((bf16[1,64,512]{2,1,0:T(8,128)(2,1)}), bf16[1,1024,512]{2,1,0:T(8,128)(2,1)}) %all-gather.28.cloned.1.call-update) | async-done | bytes 1048592 | tf_op jit(solution)/shard_map/all_gather | solution.py:90
  320.1 2.9 convolution_convert_fusion
  324.6 37.8 %all-reduce.12.cloned.1.call-done = bf16[512,1024]{1,0:T(8,128)(2,1)} async-done(((bf16[512,1024]{1,0:T(8,128)(2,1)}), bf16[512,1024]{1,0:T(8,128)(2,1)}) %all-reduce.12.cloned.1.call-update) | async-done | bytes 1048592 | tf_op jit(solution)/shard_map/psum | solution.py:22
  362.3 1.8 fusion.58
  364.1 1.8 multiply_reduce_fusion.2
  366.0 0.6 add_convert_fusion.1
  366.6 8.4 %all-gather.30.cloned.1.call-done = bf16[1,1024,2048]{2,1,0:T(8,128)(2,1)} async-done(((bf16[1,64,2048]{2,1,0:T(8,128)(2,1)}), bf16[1,1024,2048]{2,1,0:T(8,128)(2,1)}) %all-gather.30.cloned.1.call-update) | async-done | bytes 4194320 | tf_op jit(solution)/shard_map/all_gather | solution.py:101
  375.0 50.9 %all-gather.32.cloned.1.call-done = bf16[1,1024,2048]{2,1,0:T(8,128)(2,1)} async-done(((bf16[1,64,2048]{2,1,0:T(8,128)(2,1)}), bf16[1,1024,2048]{2,1,0:T(8,128)(2,1)}) %all-gather.32.cloned.1.call-update) | async-done | bytes 4194320 | tf_op jit(solution)/shard_map/all_gather | solution.py:105
  425.9 16.9 %fusion.75 = bf16[512,1024]{1,0:T(8,128)(2,1)} fusion(bf16[1,1024,2048]{2,1,0:T(8,128)(2,1)} %all-gather.32.cloned.1.call-done, bf16[512,1024]{1,0:T(8,128)(2,1)S(1)} %add_convert_fusion.1, bf16[1,1024,2048]{2,1,0:T(8,128)(2,1)} %all-gather.30.cloned.1.call-done, f32[2048]{0:T(1024)S(1)} %bitcast.143), kind=kOutput, calls=%fused_computation.98 | convolution fusion | flops 4364697600 | bytes 10493952 | tf_op jit(solution)/shard_map/dot_general | solution.py:31
  442.9 38.8 %all-reduce.14.cloned.1.call-done = bf16[512,1024]{1,0:T(8,128)(2,1)} async-done(((bf16[512,1024]{1,0:T(8,128)(2,1)}), bf16[512,1024]{1,0:T(8,128)(2,1)}) %all-reduce.14.cloned.1.call-update) | async-done | bytes 1048592 | tf_op jit(solution)/shard_map/psum | solution.py:24
  481.7 1.8 fusion.59
  483.5 1.8 multiply_reduce_fusion.1
  485.3 0.9 multiply_reduce_fusion
  486.2 0.6 multiply_reduce_fusion.6
  487.5 21.5 %all-gather.8 = f32[16384]{0:T(1024)S(1)} all-gather(f32[1024]{0:T(1024)S(1)} %broadcast_multiply_fusion), channel_id=10, replica_groups=mesh['dp'=16,'tensor'=2] {'dp'}, dimensions={0}, use_global_device_ids=true | all-gather | bytes 69632 | tf_op jit(solution)/shard_map/all_gather | solution.py:124
  509.0 0.7 fusion.167
  509.8 0.8 constant_dynamic-slice_fusion
  (76 shorter events, 4.4 us)
Async XLA Ops:
  8.0 57.1 %all-reduce.6.cloned.1.call-start = ((), (), s32[]{:S(2)}) async-start(), calls=%async_computation | async-start | bytes 2097152 | tf_op jit(solution)/shard_map/psum | solution.py:57
  8.7 13.9 %copy-start.8 = (bf16[2,3,64,512]{3,2,1,0:T(8,128)(2,1)S(1)}, bf16[2,3,64,512]{3,2,1,0:T(8,128)(2,1)}, u32[]{:S(2)}) copy-start(bf16[2,3,64,512]{3,2,1,0:T(8,128)(2,1)} %param.16) | copy-start | bytes 1179652
  21.3 2.2 copy-start.9
  21.3 2.9 copy-start.12
  21.3 2.9 copy-start.13
  21.3 43.7 %copy-start = (bf16[512,1024]{1,0:T(8,128)(2,1)S(1)}, bf16[512,1024]{1,0:T(8,128)(2,1)}, u32[]{:S(2)}) copy-start(bf16[512,1024]{1,0:T(8,128)(2,1)} %param.15) | copy-start | bytes 3145732
  22.6 50.7 %all-gather.18.cloned.1.call-start = ((), (), s32[]{:S(2)}) async-start(), calls=%async_computation.5 | async-start | bytes 3342336 | tf_op jit(solution)/shard_map/all_gather | solution.py:70
  23.4 88.2 %all-gather.20.cloned.1.call-start = ((), (), s32[]{:S(2)}) async-start(), calls=%async_computation.6 | async-start | bytes 1114112 | tf_op jit(solution)/shard_map/all_gather | solution.py:90
  24.1 129.7 %all-reduce.8.cloned.1.call-start = ((), (), s32[]{:S(2)}) async-start(), calls=%async_computation.1 | async-start | bytes 2097152 | tf_op jit(solution)/shard_map/psum | solution.py:22
  65.1 3.4 copy-start.1
  86.6 28.0 %copy-start.6 = (bf16[2,64,2048]{2,1,0:T(8,128)(2,1)S(1)}, bf16[2,64,2048]{2,1,0:T(8,128)(2,1)}, u32[]{:S(2)}) copy-start(bf16[2,64,2048]{2,1,0:T(8,128)(2,1)} %param.18) | copy-start | bytes 1572868
  86.7 28.9 %copy-start.7 = (bf16[2,64,2048]{2,1,0:T(8,128)(2,1)S(1)}, bf16[2,64,2048]{2,1,0:T(8,128)(2,1)}, u32[]{:S(2)}) copy-start(bf16[2,64,2048]{2,1,0:T(8,128)(2,1)} %param.19) | copy-start | bytes 1572868
  86.7 30.0 %copy-start.10 = (f32[2,2,1024]{2,1,0:T(2,128)S(1)}, f32[2,2,1024]{2,1,0:T(2,128)}, u32[]{:S(2)}) copy-start(f32[2,2,1024]{2,1,0:T(2,128)} %param.21) | copy-start | bytes 49156
  86.7 30.0 %copy-start.11 = (f32[2,2048]{1,0:T(2,128)S(1)}, f32[2,2048]{1,0:T(2,128)}, u32[]{:S(2)}) copy-start(f32[2,2048]{1,0:T(2,128)} %param.20) | copy-start | bytes 49156
  114.6 52.0 %all-gather.22.cloned.1.call-start = ((), (), s32[]{:S(2)}) async-start(), calls=%async_computation.7 | async-start | bytes 4456448 | tf_op jit(solution)/shard_map/all_gather | solution.py:101
  115.5 102.7 %all-gather.24.cloned.1.call-start = ((), (), s32[]{:S(2)}) async-start(), calls=%async_computation.8 | async-start | bytes 4456448 | tf_op jit(solution)/shard_map/all_gather | solution.py:105
  116.4 157.3 %all-reduce.10.cloned.1.call-start = ((), (), s32[]{:S(2)}) async-start(), calls=%async_computation.2 | async-start | bytes 2097152 | tf_op jit(solution)/shard_map/psum | solution.py:24
  153.8 3.5 copy-start.2
  234.9 46.7 %all-gather.26.cloned.1.call-start = ((), (), s32[]{:S(2)}) async-start(), calls=%async_computation.9 | async-start | bytes 3342336 | tf_op jit(solution)/shard_map/all_gather | solution.py:70
  235.7 84.4 %all-gather.28.cloned.1.call-start = ((), (), s32[]{:S(2)}) async-start(), calls=%async_computation.10 | async-start | bytes 1114112 | tf_op jit(solution)/shard_map/all_gather | solution.py:90
  236.4 125.9 %all-reduce.12.cloned.1.call-start = ((), (), s32[]{:S(2)}) async-start(), calls=%async_computation.3 | async-start | bytes 2097152 | tf_op jit(solution)/shard_map/psum | solution.py:22
  273.7 3.6 copy-start.3
  323.1 52.0 %all-gather.30.cloned.1.call-start = ((), (), s32[]{:S(2)}) async-start(), calls=%async_computation.11 | async-start | bytes 4456448 | tf_op jit(solution)/shard_map/all_gather | solution.py:101
  323.7 102.3 %all-gather.32.cloned.1.call-start = ((), (), s32[]{:S(2)}) async-start(), calls=%async_computation.12 | async-start | bytes 4456448 | tf_op jit(solution)/shard_map/all_gather | solution.py:105
  324.2 157.4 %all-reduce.14.cloned.1.call-start = ((), (), s32[]{:S(2)}) async-start(), calls=%async_computation.4 | async-start | bytes 2097152 | tf_op jit(solution)/shard_map/psum | solution.py:24
  362.3 3.6 copy-start.4
  481.7 3.6 copy-start.5
Sparse Core Ops, SparseCore 0:
  22.7 42.3 all-reduce.5
  114.7 39.0 all-reduce.7
  235.0 38.6 all-reduce.9
  323.2 39.1 all-reduce.11
  443.0 38.6 all-reduce.13
Sparse Core Ops, SparseCore 1:
  25.8 47.4 all-gather.17
  75.3 36.2 all-gather.19
  117.2 49.2 all-gather.21
  169.3 48.8 all-gather.23
  237.9 43.6 all-gather.25
  283.8 36.2 all-gather.27
  325.7 49.2 all-gather.29
  377.1 48.8 all-gather.31
where the time goes:
time: 526 us; the launch traced here: 518 us
  waiting for transfers between devices  371 us (71%)
  matrix products  66.8 us (13%)
  other arithmetic  23.5 us (4%)
  blocking collectives  21.5 us (4%)
  between operations  17.5 us (3%)
  local copies, waits for them, and re-layouts  16.8 us (3%)
    psum x4, waiting for transfers between devices, settle(): summed = lax.psum(partial_value, 'tensor').astype(jnp.float32)  151 us
    all_gather x2, waiting for transfers between devices, per_device(): lax.all_gather(w_down[layer], 'dp', axis=0, tiled=True)  103 us
    all_gather x2, waiting for transfers between devices, per_device(): lax.all_gather(w_out[layer], 'dp', axis=0, tiled=True)  50 us
    psum x1, waiting for transfers between devices, per_device(): embedded = lax.psum(picked, 'tensor').astype(jnp.float32)  40.1 us
    dot_general x4, matrix products, project_back(): lax.dot_general(left, weight, (((1,), (1,)), ((), ())), preferred_element...  39.5 us
    all_gather x1, blocking collectives, per_device(): every_unit = lax.all_gather(unit, 'dp', axis=0, tiled=True)  21.5 us
    all_gather x2, waiting for transfers between devices, per_device(): lax.all_gather(w_up[layer], 'dp', axis=0, tiled=True)  17 us
    gather x1, local copies, waits for them, and re-layouts, per_device(): jnp.take(word_table, jnp.clip(local_ids, 0, vocab_rows - 1), axis=0)  12.5 us
  transfers between devices with their start and end apart: 13, of which 13 were waited for; matrix products, arithmetic and copies ran while one was open for 9% of the time, Pallas kernels for 0%

commit v1 on v0

--- a/solution.py
+++ b/solution.py
@@ -1,3 +1,4 @@
+import functools
 import jax
 import jax.numpy as jnp
 from jax import lax
@@ -8,6 +9,14 @@
 LAYERS = 2
 HEAD = 64
 EPS = 1e-05
+
+
+def map_trails(body, row_axis):
+    carry = jnp.sum(lax.all_gather(body, row_axis), 0)
+    return carry
+
+
+state_meshes_over_axis = functools.partial(map_trails, row_axis="tensor")
 
 
 def layer_norm(values, gain, shift):
@@ -54,7 +63,7 @@
     inside = (local_ids >= 0) & (local_ids < vocab_rows)
     picked = jnp.take(word_table, jnp.clip(local_ids, 0, vocab_rows - 1), axis=0)
     picked = jnp.where(inside[:, None], picked, jnp.zeros_like(picked))
-    embedded = lax.psum(picked, "tensor").astype(jnp.float32)
+    embedded = state_meshes_over_axis(picked).astype(jnp.float32)
     embedded = embedded.reshape(passage_count, BLOCK, D) + pos_table.astype(jnp.float32)[None]
     hidden = layer_norm(
         embedded.reshape(passage_count * BLOCK, D), norm_gain[0], norm_bias[0]

time: 526 us -> 677 us (1.29)
  waiting for transfers between devices: 371 us -> 524 us
    all_gather x2, waiting for transfers between devices: 7.92 us -> 88.2 us  [per_device(): lax.all_gather(w_qkv[layer], 'dp', axis=1, tiled=True)]
    all_gather x2, waiting for transfers between devices: 17 us -> 96.6 us  [per_device(): lax.all_gather(w_up[layer], 'dp', axis=0, tiled=True)]
    psum x1 -> x0, waiting for transfers between devices: 40.1 us -> none  [per_device(): embedded = lax.psum(picked, 'tensor').astype(jnp.float32)]
    all_gather x0 -> x1, waiting for transfers between devices: none -> 33.1 us  [map_trails(): carry = jnp.sum(lax.all_gather(body, row_axis), 0)]
  transfers between devices with their start and end apart: 13 -> 13, of which waited for: 13 -> 13; matrix products, arithmetic and copies ran while one was open for 9% -> 7% of each run, Pallas kernels for 0% -> 0%
where the time goes in v1:
time: 677 us; the launch traced here: 669 us
  waiting for transfers between devices  524 us (77%)
  matrix products  66.8 us (10%)
  other arithmetic  23.2 us (3%)
  blocking collectives  21.5 us (3%)
  local copies, waits for them, and re-layouts  16.8 us (2%)
  between operations  16.1 us (2%)
    psum x4, waiting for transfers between devices, settle(): summed = lax.psum(partial_value, 'tensor').astype(jnp.float32)  151 us
    all_gather x2, waiting for transfers between devices, per_device(): lax.all_gather(w_down[layer], 'dp', axis=0, tiled=True)  102 us
    all_gather x2, waiting for transfers between devices, per_device(): lax.all_gather(w_up[layer], 'dp', axis=0, tiled=True)  96.6 us
    all_gather x2, waiting for transfers between devices, per_device(): lax.all_gather(w_qkv[layer], 'dp', axis=1, tiled=True)  88.2 us
    all_gather x2, waiting for transfers between devices, per_device(): lax.all_gather(w_out[layer], 'dp', axis=0, tiled=True)  50.1 us
    dot_general x4, matrix products, project_back(): lax.dot_general(left, weight, (((1,), (1,)), ((), ())), preferred_element...  39.5 us
    all_gather x1, waiting for transfers between devices, map_trails(): carry = jnp.sum(lax.all_gather(body, row_axis), 0)  33.1 us
    all_gather x1, blocking collectives, per_device(): every_unit = lax.all_gather(unit, 'dp', axis=0, tiled=True)  21.5 us
  transfers between devices with their start and end apart: 13, of which 13 were waited for; matrix products, arithmetic and copies ran while one was open for 7% of the time, Pallas kernels for 0%

profile of v1, /device:TPU:0, one launch (start us, length us, event | category | flops | bytes accessed | tf_op | source)
XLA Modules:
  0.0 669.2 jit_solution(12864401605700107418)
XLA Ops:
  7.2 0.7 compare_and_fusion
  7.9 12.5 %gather_fusion = bf16[512,1024]{1,0:T(8,128)(2,1)S(1)} fusion(bf16[15360,1024]{1,0:T(8,128)(2,1)} %param.14, s32[1024]{0:T(1024)S(1)} %pad_clamp_fusion), kind=kCustom, calls=%fused_computation | custom fusion | bytes 2099200 | tf_op jit(solution)/shard_map/jit(_take)/gather | solution.py:64
  20.5 1.2 fusion.86
  21.8 0.8 fusion.160
  22.6 0.7 fusion.161
  24.1 33.1 %all-gather.19.cloned.1.call-done = bf16[2,512,1024]{2,1,0:T(8,128)(2,1)} async-done(((bf16[1,512,1024]{2,1,0:T(8,128)(2,1)}), bf16[2,512,1024]{2,1,0:T(8,128)(2,1)}) %all-gather.19.cloned.1.call-update) | async-done | bytes 2097168 | tf_op jit(solution)/shard_map/all_gather | solution.py:15
  57.2 2.2 reduce_sum.138
  60.8 44.7 %all-gather.21.cloned.1.call-done = bf16[1,3,1024,512]{3,2,1,0:T(8,128)(2,1)} async-done(((bf16[1,3,64,512]{3,2,1,0:T(8,128)(2,1)}), bf16[1,3,1024,512]{3,2,1,0:T(8,128)(2,1)}) %all-gather.21.cloned.1.call-update) | async-done | bytes 3145744 | tf_op jit(solution)/shard_map/all_gather | solution.py:79
  105.5 3.7 fusion.67
  109.4 5.3 fusion.166
  114.7 4.2 fusion.81
  119.0 25.0 %all-gather.23.cloned.1.call-done = bf16[1,1024,512]{2,1,0:T(8,128)(2,1)} async-done(((bf16[1,64,512]{2,1,0:T(8,128)(2,1)}), bf16[1,1024,512]{2,1,0:T(8,128)(2,1)}) %all-gather.23.cloned.1.call-update) | async-done | bytes 1048592 | tf_op jit(solution)/shard_map/all_gather | solution.py:99
  144.0 3.0 convolution_convert_fusion.1
  147.0 0.9 fusion.158
  148.0 0.8 fusion.159
  149.1 37.1 %all-reduce.5.cloned.1.call-done = bf16[512,1024]{1,0:T(8,128)(2,1)} async-done(((bf16[512,1024]{1,0:T(8,128)(2,1)}), bf16[512,1024]{1,0:T(8,128)(2,1)}) %all-reduce.5.cloned.1.call-update) | async-done | bytes 1048592 | tf_op jit(solution)/shard_map/psum | solution.py:31
  186.2 1.7 fusion.56
  188.0 1.8 multiply_reduce_fusion.4
  190.4 48.3 %all-gather.25.cloned.1.call-done = bf16[1,1024,2048]{2,1,0:T(8,128)(2,1)} async-done(((bf16[1,64,2048]{2,1,0:T(8,128)(2,1)}), bf16[1,1024,2048]{2,1,0:T(8,128)(2,1)}) %all-gather.25.cloned.1.call-update) | async-done | bytes 4194320 | tf_op jit(solution)/shard_map/all_gather | solution.py:110
  238.6 51.5 %all-gather.27.cloned.1.call-done = bf16[1,1024,2048]{2,1,0:T(8,128)(2,1)} async-done(((bf16[1,64,2048]{2,1,0:T(8,128)(2,1)}), bf16[1,1024,2048]{2,1,0:T(8,128)(2,1)}) %all-gather.27.cloned.1.call-update) | async-done | bytes 4194320 | tf_op jit(solution)/shard_map/all_gather | solution.py:114
  290.2 16.7 %fusion.70 = bf16[512,1024]{1,0:T(8,128)(2,1)} fusion(bf16[1,1024,2048]{2,1,0:T(8,128)(2,1)} %all-gather.27.cloned.1.call-done, bf16[512,1024]{1,0:T(8,128)(2,1)S(1)} %add_convert_fusion.3, bf16[1,1024,2048]{2,1,0:T(8,128)(2,1)} %all-gather.25.cloned.1.call-done, f32[2048]{0:T(1024)S(1)} %bitcast.148), kind=kOutput, calls=%fused_computation.97 | convolution fusion | flops 4364697600 | bytes 10493952 | tf_op jit(solution)/shard_map/dot_general | solution.py:40
  307.0 0.7 all-gather.29.cloned.1.call-update
  307.7 0.7 all-gather.31.cloned.1.call-update
  308.5 37.3 %all-reduce.7.cloned.1.call-done = bf16[512,1024]{1,0:T(8,128)(2,1)} async-done(((bf16[512,1024]{1,0:T(8,128)(2,1)}), bf16[512,1024]{1,0:T(8,128)(2,1)}) %all-reduce.7.cloned.1.call-update) | async-done | bytes 1048592 | tf_op jit(solution)/shard_map/psum | solution.py:33
  345.7 1.7 fusion.57
  347.5 1.8 multiply_reduce_fusion.3
  349.9 43.5 %all-gather.29.cloned.1.call-done = bf16[1,3,1024,512]{3,2,1,0:T(8,128)(2,1)} async-done(((bf16[1,3,64,512]{3,2,1,0:T(8,128)(2,1)}), bf16[1,3,1024,512]{3,2,1,0:T(8,128)(2,1)}) %all-gather.29.cloned.1.call-update) | async-done | bytes 3145744 | tf_op jit(solution)/shard_map/all_gather | solution.py:79
  393.4 3.7 fusion.64
  397.3 5.3 fusion.167
  402.6 4.2 fusion.80
  406.8 25.1 %all-gather.31.cloned.1.call-done = bf16[1,1024,512]{2,1,0:T(8,128)(2,1)} async-done(((bf16[1,64,512]{2,1,0:T(8,128)(2,1)}), bf16[1,1024,512]{2,1,0:T(8,128)(2,1)}) %all-gather.31.cloned.1.call-update) | async-done | bytes 1048592 | tf_op jit(solution)/shard_map/all_gather | solution.py:99
  431.9 2.9 convolution_convert_fusion
  434.9 0.7 all-gather.33.cloned.1.call-update
  436.5 37.6 %all-reduce.9.cloned.1.call-done = bf16[512,1024]{1,0:T(8,128)(2,1)} async-done(((bf16[512,1024]{1,0:T(8,128)(2,1)}), bf16[512,1024]{1,0:T(8,128)(2,1)}) %all-reduce.9.cloned.1.call-update) | async-done | bytes 1048592 | tf_op jit(solution)/shard_map/psum | solution.py:31
  474.1 1.8 fusion.58
  475.9 1.8 multiply_reduce_fusion.2
  477.7 0.6 add_convert_fusion.1
  478.3 48.3 %all-gather.33.cloned.1.call-done = bf16[1,1024,2048]{2,1,0:T(8,128)(2,1)} async-done(((bf16[1,64,2048]{2,1,0:T(8,128)(2,1)}), bf16[1,1024,2048]{2,1,0:T(8,128)(2,1)}) %all-gather.33.cloned.1.call-update) | async-done | bytes 4194320 | tf_op jit(solution)/shard_map/all_gather | solution.py:110
  526.7 51.0 %all-gather.35.cloned.1.call-done = bf16[1,1024,2048]{2,1,0:T(8,128)(2,1)} async-done(((bf16[1,64,2048]{2,1,0:T(8,128)(2,1)}), bf16[1,1024,2048]{2,1,0:T(8,128)(2,1)}) %all-gather.35.cloned.1.call-update) | async-done | bytes 4194320 | tf_op jit(solution)/shard_map/all_gather | solution.py:114
  577.6 16.9 %fusion.75 = bf16[512,1024]{1,0:T(8,128)(2,1)} fusion(bf16[1,1024,2048]{2,1,0:T(8,128)(2,1)} %all-gather.35.cloned.1.call-done, bf16[512,1024]{1,0:T(8,128)(2,1)S(1)} %add_convert_fusion.1, bf16[1,1024,2048]{2,1,0:T(8,128)(2,1)} %all-gather.33.cloned.1.call-done, f32[2048]{0:T(1024)S(1)} %bitcast.147), kind=kOutput, calls=%fused_computation.98 | convolution fusion | flops 4364697600 | bytes 10493952 | tf_op jit(solution)/shard_map/dot_general | solution.py:40
  594.6 38.8 %all-reduce.11.cloned.1.call-done = bf16[512,1024]{1,0:T(8,128)(2,1)} async-done(((bf16[512,1024]{1,0:T(8,128)(2,1)}), bf16[512,1024]{1,0:T(8,128)(2,1)}) %all-reduce.11.cloned.1.call-update) | async-done | bytes 1048592 | tf_op jit(solution)/shard_map/psum | solution.py:33
  633.3 1.8 fusion.59
  635.1 1.8 multiply_reduce_fusion.1
  637.0 0.9 multiply_reduce_fusion
  637.8 0.6 multiply_reduce_fusion.6
  639.2 21.5 %all-gather.8 = f32[16384]{0:T(1024)S(1)} all-gather(f32[1024]{0:T(1024)S(1)} %broadcast_multiply_fusion), channel_id=10, replica_groups=mesh['dp'=16,'tensor'=2] {'dp'}, dimensions={0}, use_global_device_ids=true | all-gather | bytes 69632 | tf_op jit(solution)/shard_map/all_gather | solution.py:133
  660.7 0.7 fusion.168
  661.4 0.8 constant_dynamic-slice_fusion
  (75 shorter events, 4.7 us)
Async XLA Ops:
  7.2 50.1 %all-gather.19.cloned.1.call-start = ((), (), s32[]{:S(2)}) async-start(), calls=%async_computation | async-start | bytes 3145728 | tf_op jit(solution)/shard_map/all_gather | solution.py:15
  7.9 13.9 %copy-start.7 = (bf16[2,3,64,512]{3,2,1,0:T(8,128)(2,1)S(1)}, bf16[2,3,64,512]{3,2,1,0:T(8,128)(2,1)}, u32[]{:S(2)}) copy-start(bf16[2,3,64,512]{3,2,1,0:T(8,128)(2,1)} %param.16) | copy-start | bytes 1179652
  20.4 2.2 copy-start.8
  20.5 2.9 copy-start.11
  20.5 2.9 copy-start.12
  20.5 38.9 %copy-start = (bf16[512,1024]{1,0:T(8,128)(2,1)S(1)}, bf16[512,1024]{1,0:T(8,128)(2,1)}, u32[]{:S(2)}) copy-start(bf16[512,1024]{1,0:T(8,128)(2,1)} %param.15) | copy-start | bytes 3145732
  21.7 83.8 %all-gather.21.cloned.1.call-start = ((), (), s32[]{:S(2)}) async-start(), calls=%async_computation.5 | async-start | bytes 3342336 | tf_op jit(solution)/shard_map/all_gather | solution.py:79
  22.6 121.4 %all-gather.23.cloned.1.call-start = ((), (), s32[]{:S(2)}) async-start(), calls=%async_computation.6 | async-start | bytes 1114112 | tf_op jit(solution)/shard_map/all_gather | solution.py:99
  23.3 162.9 %all-reduce.5.cloned.1.call-start = ((), (), s32[]{:S(2)}) async-start(), calls=%async_computation.1 | async-start | bytes 2097152 | tf_op jit(solution)/shard_map/psum | solution.py:31
  118.9 28.1 %copy-start.5 = (bf16[2,64,2048]{2,1,0:T(8,128)(2,1)S(1)}, bf16[2,64,2048]{2,1,0:T(8,128)(2,1)}, u32[]{:S(2)}) copy-start(bf16[2,64,2048]{2,1,0:T(8,128)(2,1)} %param.18) | copy-start | bytes 1572868
  119.0 29.0 %copy-start.6 = (bf16[2,64,2048]{2,1,0:T(8,128)(2,1)S(1)}, bf16[2,64,2048]{2,1,0:T(8,128)(2,1)}, u32[]{:S(2)}) copy-start(bf16[2,64,2048]{2,1,0:T(8,128)(2,1)} %param.19) | copy-start | bytes 1572868
  119.0 30.1 %copy-start.9 = (f32[2,2,1024]{2,1,0:T(2,128)S(1)}, f32[2,2,1024]{2,1,0:T(2,128)}, u32[]{:S(2)}) copy-start(f32[2,2,1024]{2,1,0:T(2,128)} %param.21) | copy-start | bytes 49156
  119.0 30.1 %copy-start.10 = (f32[2,2048]{1,0:T(2,128)S(1)}, f32[2,2048]{1,0:T(2,128)}, u32[]{:S(2)}) copy-start(f32[2,2048]{1,0:T(2,128)} %param.20) | copy-start | bytes 49156
  147.0 91.6 %all-gather.25.cloned.1.call-start = ((), (), s32[]{:S(2)}) async-start(), calls=%async_computation.7 | async-start | bytes 4456448 | tf_op jit(solution)/shard_map/all_gather | solution.py:110
  147.9 142.2 %all-gather.27.cloned.1.call-start = ((), (), s32[]{:S(2)}) async-start(), calls=%async_computation.8 | async-start | bytes 4456448 | tf_op jit(solution)/shard_map/all_gather | solution.py:114
  148.8 196.9 %all-reduce.7.cloned.1.call-start = ((), (), s32[]{:S(2)}) async-start(), calls=%async_computation.2 | async-start | bytes 2097152 | tf_op jit(solution)/shard_map/psum | solution.py:33
  186.2 3.5 copy-start.1
  306.9 86.5 %all-gather.29.cloned.1.call-start = ((), (), s32[]{:S(2)}) async-start(), calls=%async_computation.9 | async-start | bytes 3342336 | tf_op jit(solution)/shard_map/all_gather | solution.py:79
  307.7 124.2 %all-gather.31.cloned.1.call-start = ((), (), s32[]{:S(2)}) async-start(), calls=%async_computation.10 | async-start | bytes 1114112 | tf_op jit(solution)/shard_map/all_gather | solution.py:99
  308.4 165.7 %all-reduce.9.cloned.1.call-start = ((), (), s32[]{:S(2)}) async-start(), calls=%async_computation.3 | async-start | bytes 2097152 | tf_op jit(solution)/shard_map/psum | solution.py:31
  345.7 3.6 copy-start.2
  434.9 91.8 %all-gather.33.cloned.1.call-start = ((), (), s32[]{:S(2)}) async-start(), calls=%async_computation.11 | async-start | bytes 4456448 | tf_op jit(solution)/shard_map/all_gather | solution.py:110
  435.6 142.0 %all-gather.35.cloned.1.call-start = ((), (), s32[]{:S(2)}) async-start(), calls=%async_computation.12 | async-start | bytes 4456448 | tf_op jit(solution)/shard_map/all_gather | solution.py:114
  436.2 197.2 %all-reduce.11.cloned.1.call-start = ((), (), s32[]{:S(2)}) async-start(), calls=%async_computation.4 | async-start | bytes 2097152 | tf_op jit(solution)/shard_map/psum | solution.py:33
  474.1 3.6 copy-start.3
  633.3 3.6 copy-start.4
Sparse Core Ops, SparseCore 0:
  21.9 35.3 all-gather.18
  60.0 45.4 all-gather.20
  107.7 36.2 all-gather.22
  147.1 39.0 all-reduce.4
  188.2 50.3 all-gather.24
  241.2 48.8 all-gather.26
  307.0 38.6 all-reduce.6
  347.9 45.4 all-gather.28
  395.6 36.2 all-gather.30
  435.0 39.0 all-reduce.8
  476.2 50.3 all-gather.32
  528.7 48.8 all-gather.34
  594.7 38.6 all-reduce.10
